TPU v7x, 512 devices: a whole 4x4x16 slice. The times are simulated.
512 devices in a mesh: fsdp: 16 (over x, z_hi), tensor: 8 (over z_lo, core), pool: 4 (over y).
Axes of the slice: x: 4, y: 4, z: 16 (z_hi: 4, z_lo: 4; z = z_hi * 4 + z_lo), core: 2. Of those that a mesh axis runs over, the one named last changes fastest.
Arguments:
- hidden: bfloat16 [32768, 5120], P(('fsdp', 'pool'), 'tensor'), may hold values from -6 to 6
- queries: bfloat16 [32768, 5120], P(('fsdp', 'pool'), 'tensor'), may hold values from -200 to 200
- cotangent: bfloat16 [32768, 5120], P(('fsdp', 'pool'), 'tensor'), may hold values from -6 to 6
- segment: int32 [64, 512], P(('fsdp', 'pool')), may hold values from 0 to 15, never falling along the last dimension, each value on 1 to 384 neighbouring positions
- clip_mask: int32 [32768], P(('fsdp', 'pool')), may hold values 0 or 1
- rewards: float32 [1024], P(('fsdp', 'pool')), may hold values from 0 to 1
- seq_order: int32 [1024], P(('fsdp', 'pool')), may hold values from 0 to 1023, each once
- kv_weight: float32 [5120, 2, 1024], P('fsdp', None, 'tensor'), may hold values from -0.078125 to 0.078125
- moment_one: float32 [5120, 2, 1024], P('fsdp', None, 'tensor'), may hold values from -60 to 60
- moment_two: float32 [5120, 2, 1024], P('fsdp', None, 'tensor'), may hold values from 1 to 10000
- dec_hidden: bfloat16 [512, 4, 5120], P(('fsdp', 'pool')), may hold values from -6 to 6
- dec_queries: bfloat16 [512, 4, 5120], P(('fsdp', 'pool'), None, 'tensor'), may hold values from -200 to 200
- kv_cache: bfloat16 [512, 256, 2, 1024], P(('fsdp', 'pool'), None, None, 'tensor'), may hold values from -6 to 6
- cache_len: int32 [512], P(('fsdp', 'pool')), may hold values from 1 to 256
Outputs:
- new_weight: float32 [5120, 2, 1024], P('fsdp', None, 'tensor')
- new_moment_one: float32 [5120, 2, 1024], P('fsdp', None, 'tensor')
- new_moment_two: float32 [5120, 2, 1024], P('fsdp', None, 'tensor')
- dec_out: bfloat16 [512, 4, 5120], P(('fsdp', 'pool'), None, 'tensor')
Inputs may be any that keep to these rules, and one draw needn't show every extreme that they name: `segment`: each row never falls; every sequence number of a row has 1 to 384 tokens. `seq_order`: each place once.
All inputs are finite; a program needn't handle non-finite values. No bound on the sum of `clip_mask` on one device may be relied on, other than what follows from the above.
Results may differ from a plain program's by a relative error of at most 0.014.
The roundings to bfloat16 on the way count: a program that leaves them out, or rounds other values in their place, can miss the bound.
Values may be sent and summed in bfloat16 or wider, within the bound.
A program may use at most 64 MiB of HBM per device.

v0:
```python
import math
import jax
import jax.numpy as jnp
from jax import lax
from jax.sharding import Mesh
from jax.sharding import PartitionSpec as P

D = 5120
QH = 40
KVH = 8
HD = 128
GROUP = 16
FSDP = ("fsdp_0", "fsdp_1")
FSDP_POOL = ("fsdp_0", "fsdp_1", "pool")
beta_one = 0.9
beta_two = 0.999
learn_rate = 0.001
weight_decay = 0.1
adam_epsilon = 1e-08
adam_step = 10.0
variance_floor = 0.04
masked_score = -1e30


def from_everyone(shard, axis):
    count = lax.axis_size(axis)
    return lax.all_to_all(
        jnp.broadcast_to(shard[None], (count, *shard.shape)), axis, 0, 0, tiled=True
    )


def of_everyone(shard, axis):
    everything = from_everyone(shard, axis)
    return jnp.sum(everything, axis=0)


def sum_by_axis(terms, axes):
    so_far = terms.astype(jnp.bfloat16)
    for axis in axes:
        so_far = lax.psum_scatter(so_far, axis, scatter_dimension=0, tiled=True)
    return so_far.astype(jnp.float32)


def cut_along(shard, dim, count):
    before, after = (shard.shape[:dim], shard.shape[dim + 1 :])
    return jnp.moveaxis(shard.reshape(*before, count, -1, *after), dim, 0)


def summed_on_arrival(shard, axis, dim):
    pieces = cut_along(shard, dim, lax.axis_size(axis))
    arrived = lax.all_to_all(pieces, axis, split_axis=0, concat_axis=0, tiled=True)
    return arrived.sum(axis=0)


def learner_grads(keys_values, queries, cotangent, segment, coefficient):
    block_rows = queries.shape[0]
    head_size = queries.shape[3]
    score_scale = 1.0 / math.sqrt(head_size)
    key_rows = keys_values[:, 0]
    value_rows = keys_values[:, 1]
    scores = (
        jnp.einsum("thrd,uhd->hrtu", queries, key_rows, preferred_element_type=jnp.float32)
        * score_scale
    )
    places = jnp.arange(block_rows)
    allowed = (segment[:, None] == segment[None, :]) & (places[None, :] <= places[:, None])
    scores = jnp.where(allowed, scores, masked_score)
    row_max = jnp.max(scores, axis=-1, keepdims=True)
    weights = jnp.exp(scores - row_max)
    attention = weights / jnp.sum(weights, axis=-1, keepdims=True)
    attention_low = attention.astype(jnp.bfloat16)
    upstream = (coefficient[:, None, None, None] * cotangent.astype(jnp.float32)).astype(
        jnp.bfloat16
    )
    grad_prob = jnp.einsum(
        "thrd,uhd->hrtu", upstream, value_rows, preferred_element_type=jnp.float32
    )
    row_inner = jnp.sum(attention * grad_prob, axis=-1, keepdims=True)
    grad_score = (attention * (grad_prob - row_inner) * score_scale).astype(jnp.bfloat16)
    grad_values = jnp.einsum(
        "hrtu,thrd->uhd", attention_low, upstream, preferred_element_type=jnp.float32
    )
    grad_keys = jnp.einsum(
        "hrtu,thrd->uhd", grad_score, queries, preferred_element_type=jnp.float32
    )
    return jnp.stack([grad_keys, grad_values], axis=1).astype(jnp.bfloat16)


def decode_attend(queries, cache, fresh, lengths):
    head_size = queries.shape[4]
    steps_here = queries.shape[1]
    capacity = cache.shape[1]
    score_scale = 1.0 / math.sqrt(head_size)
    cached = (
        jnp.einsum("bshqd,blhd->bshql", queries, cache[:, :, 0], preferred_element_type=jnp.float32)
        * score_scale
    )
    recent = (
        jnp.einsum("bshqd,bjhd->bshqj", queries, fresh[:, :, 0], preferred_element_type=jnp.float32)
        * score_scale
    )
    live = jnp.arange(capacity)[None, :] < lengths[:, None]
    cached = jnp.where(live[:, None, None, None, :], cached, masked_score)
    before = jnp.arange(steps_here)[None, :] <= jnp.arange(steps_here)[:, None]
    recent = jnp.where(before[None, :, None, None, :], recent, masked_score)
    row_max = jnp.maximum(
        jnp.max(cached, axis=-1, keepdims=True), jnp.max(recent, axis=-1, keepdims=True)
    )
    cached_exp = jnp.exp(cached - row_max)
    recent_exp = jnp.exp(recent - row_max)
    total = jnp.sum(cached_exp, axis=-1, keepdims=True) + jnp.sum(
        recent_exp, axis=-1, keepdims=True
    )
    cached_low = (cached_exp / total).astype(jnp.bfloat16)
    recent_low = (recent_exp / total).astype(jnp.bfloat16)
    output = jnp.einsum(
        "bshql,blhd->bshqd", cached_low, cache[:, :, 1], preferred_element_type=jnp.float32
    )
    output = output + jnp.einsum(
        "bshqj,bjhd->bshqd", recent_low, fresh[:, :, 1], preferred_element_type=jnp.float32
    )
    return output.astype(jnp.bfloat16).reshape(queries.shape[0], steps_here, -1)


def body(
    hidden,
    queries,
    cotangent,
    segment,
    clip_mask,
    rewards,
    seq_order,
    kv_weight,
    moment_one,
    moment_two,
    dec_hidden,
    dec_queries,
    kv_cache,
    cache_len,
):
    block_rows = hidden.shape[0]
    kv_width = kv_weight.shape[2]
    heads_here = kv_width // HD
    head_ratio = QH // KVH
    weight_low = kv_weight.astype(jnp.bfloat16)
    weight_full = lax.all_gather(weight_low, FSDP, axis=0, tiled=True)
    tokens_full = lax.all_gather(hidden, "tensor", axis=1, tiled=True)
    projected = jnp.dot(
        tokens_full, weight_full.reshape(D, 2 * kv_width), preferred_element_type=jnp.float32
    )
    keys_values = projected.astype(jnp.bfloat16).reshape(block_rows, 2, heads_here, HD)
    shards = lax.axis_size(FSDP) * lax.axis_size("pool")
    groups_total = rewards.shape[0] * shards // GROUP
    group_of = seq_order // GROUP
    onehot = (group_of[:, None] == jnp.arange(groups_total, dtype=jnp.int32)[None, :]).astype(
        jnp.float32
    )
    stats = jnp.stack([rewards, rewards * rewards], axis=1)
    partial_sums = jnp.sum(onehot[:, :, None] * stats[:, None, :], axis=0)
    sums = of_everyone(partial_sums, FSDP_POOL)
    mean = sums[:, 0] / GROUP
    spread = sums[:, 1] / GROUP - mean * mean
    denom = jnp.sqrt(jnp.maximum(spread, variance_floor))
    advantage = (rewards - jnp.sum(onehot * mean[None, :], axis=1)) / jnp.sum(
        onehot * denom[None, :], axis=1
    )
    local_seg = segment[0]
    member = (local_seg[:, None] == jnp.arange(rewards.shape[0], dtype=jnp.int32)[None, :]).astype(
        jnp.float32
    )
    coefficient = jnp.sum(member * advantage[None, :], axis=1) * clip_mask.astype(jnp.float32)
    query_rows = queries.reshape(block_rows, heads_here, head_ratio, HD)
    cot_rows = cotangent.reshape(block_rows, heads_here, head_ratio, HD)
    grad_kv = learner_grads(keys_values, query_rows, cot_rows, local_seg, coefficient).reshape(
        block_rows, 2 * kv_width
    )
    partial_value = jnp.einsum(
        "tc,tk->ck", tokens_full, grad_kv, preferred_element_type=jnp.float32
    )
    shard_grad = sum_by_axis(
        partial_value.reshape(kv_weight.shape[0] * lax.axis_size(FSDP), 2, kv_width), FSDP
    )
    grad = of_everyone(shard_grad, "pool")
    new_moment_one = beta_one * moment_one + (1.0 - beta_one) * grad
    new_moment_two = beta_two * moment_two + (1.0 - beta_two) * grad * grad
    first_hat = new_moment_one / (1.0 - beta_one**adam_step)
    second_hat = new_moment_two / (1.0 - beta_two**adam_step)
    new_weight = kv_weight - learn_rate * (
        first_hat / (jnp.sqrt(second_hat) + adam_epsilon) + weight_decay * kv_weight
    )
    dec_rows = dec_hidden.shape[0]
    steps_here = dec_hidden.shape[1]
    capacity = kv_cache.shape[1]
    rollout_low = new_weight.astype(jnp.bfloat16)
    columns = lax.all_to_all(dec_hidden, FSDP, split_axis=2, concat_axis=0, tiled=True)
    piece_width = columns.shape[2]
    rollout_flat = rollout_low.reshape(piece_width, 2 * kv_width)
    product = jnp.dot(
        columns.reshape(dec_rows * lax.axis_size(FSDP) * steps_here, piece_width),
        rollout_flat,
        preferred_element_type=jnp.float32,
    )
    fresh = summed_on_arrival(
        product.reshape(dec_rows * lax.axis_size(FSDP), steps_here, 2 * kv_width), FSDP, 0
    )
    fresh_low = fresh.astype(jnp.bfloat16).reshape(dec_rows, steps_here, 2, heads_here, HD)
    cache = kv_cache.reshape(dec_rows, capacity, 2, heads_here, HD)
    query_dec = dec_queries.reshape(dec_rows, steps_here, heads_here, head_ratio, HD)
    dec_out = decode_attend(query_dec, cache, fresh_low, cache_len)
    return (new_weight, new_moment_one, new_moment_two, dec_out)


def solution(mesh):
    finer = Mesh(
        mesh.devices.reshape(4, 4, mesh.shape["tensor"], mesh.shape["pool"]),
        ("fsdp_0", "fsdp_1", "tensor", "pool"),
    )
    in_specs = (
        P(FSDP_POOL, "tensor"),
        P(FSDP_POOL, "tensor"),
        P(FSDP_POOL, "tensor"),
        P(FSDP_POOL, None),
        P(FSDP_POOL),
        P(FSDP_POOL),
        P(FSDP_POOL),
        P(FSDP, None, "tensor"),
        P(FSDP, None, "tensor"),
        P(FSDP, None, "tensor"),
        P(FSDP_POOL, None, None),
        P(FSDP_POOL, None, "tensor"),
        P(FSDP_POOL, None, None, "tensor"),
        P(FSDP_POOL),
    )
    out_specs = (
        P(FSDP, None, "tensor"),
        P(FSDP, None, "tensor"),
        P(FSDP, None, "tensor"),
        P(FSDP_POOL, None, "tensor"),
    )
    return jax.shard_map(body, mesh=finer, in_specs=in_specs, out_specs=out_specs, check_vma=False)
```

profile of v0, /device:TPU:1, one launch (start us, length us, event | category | flops | bytes accessed | tf_op | source)
XLA Modules:
  0.0 462.3 jit_solution(10101156402707544405)
XLA Ops:
  7.2 1.8 convert_element_type.98
  9.0 0.7 all-gather.3.cloned.1.call-update
  9.7 0.7 multiply_bitcast_fusion.1
  10.4 0.7 pad_maximum_fusion.1
  11.1 0.7 and_select_fusion
  11.8 0.1 multiply_reduce_fusion
  11.9 0.7 reshape.300
  12.6 21.7 %all-to-all-start = ((f32[64,1,128]{2,1,0:T(1,128)}), f32[64,1,128]{2,1,0:T(1,128)S(1)}, u32[]{:S(2)}, u32[]{:S(2)}) async-start(f32[64,1,128]{2,1,0:T(1,128)} %reshape.300), calls=%async_computation | async-start | bytes 65536 | tf_op jit(solution)/shard_map/all_to_all | solution.py:27
  34.4 1.3 copy.154
  35.8 1.3 copy.157
  37.1 1.0 fusion.49
  38.1 11.9 %all-to-all-done = f32[64,1,128]{2,1,0:T(1,128)S(1)} async-done(((f32[64,1,128]{2,1,0:T(1,128)}), f32[64,1,128]{2,1,0:T(1,128)S(1)}, u32[]{:S(2)}, u32[]{:S(2)}) %all-to-all-start) | async-done | bytes 32800 | tf_op jit(solution)/shard_map/all_to_all | solution.py:27
  50.0 0.5 broadcast.178
  50.5 0.7 reduce.7
  51.2 0.1 reshape.301
  51.3 0.1 bitcast_reduce_fusion
  51.4 0.2 select_reduce_fusion.2
  51.6 0.7 subtract_divide_fusion
  52.2 0.8 select_reduce_fusion
  53.0 0.7 convert_multiply_fusion
  53.7 0.1 multiply_convert_fusion.1
  53.8 68.1 %all-gather.5.cloned.1.call-done = bf16[5120,2,128]{2,1,0:T(2,128)(2,1)} async-done(((bf16[320,2,128]{2,1,0:T(2,128)(2,1)}), bf16[5120,2,128]{2,1,0:T(2,128)(2,1)}) %all-gather.5.cloned.1.call-update) | async-done | bytes 2621456 | tf_op jit(solution)/shard_map/all_gather | solution.py:146
  122.0 66.0 %all-gather.3.cloned.1.call-done = bf16[512,5120]{1,0:T(8,128)(2,1)} async-done(((bf16[512,640]{1,0:T(8,128)(2,1)}), bf16[512,5120]{1,0:T(8,128)(2,1)}) %all-gather.3.cloned.1.call-update) | async-done | bytes 5242896 | tf_op jit(solution)/shard_map/all_gather | solution.py:147
  187.9 4.9 %fusion.20 = bf16[512,256]{0,1:T(8,128)(2,1)S(1)} fusion(bf16[512,5120]{1,0:T(8,128)(2,1)} %all-gather.3.cloned.1.call-done, bf16[640,8,2,128]{3,2,1,0:T(2,128)(2,1)} %bitcast.254), kind=kOutput, calls=%fused_computation.25 | convolution fusion | flops 1342308352 | bytes 8126464 | tf_op jit(solution)/shard_map/dot_general | solution.py:148
  192.8 1.1 fusion.6
  193.9 1.1 fusion.5
  195.0 1.7 fusion.39
  196.7 1.9 fusion
  198.6 2.4 fusion.42
  201.2 1.6 convolution_convert_fusion
  202.8 4.7 %copy.161 = bf16[5120,2,128]{2,1,0:T(2,128)(2,1)} copy(bf16[5120,2,128]{0,2,1:T(8,128)(2,1)S(1)} %bitcast.240) | data formatting | bytes 5242880 | tf_op jit(solution)/shard_map/convert_element_type | solution.py:38
  207.5 5.0 %copy.170 = bf16[8,4,5120]{0,1,2:T(4,128)(2,1)} copy(bf16[8,4,5120]{2,1,0:T(4,128)(2,1)S(1)} %copy-done.3) | data formatting | bytes 655360 | tf_op args[10]
  212.5 12.3 %reshape.302 = bf16[16,2,5120]{2,1,0:T(2,128)(2,1)} reshape(bf16[5120,4,8]{2,1,0:T(4,128)(2,1)} %bitcast.237) | data formatting | bytes 655360
  224.8 14.2 %all-to-all-start.2 = ((bf16[16,2,5120]{2,1,0:T(2,128)(2,1)}), bf16[16,2,5120]{2,1,0:T(2,128)(2,1)S(1)}, u32[]{:S(2)}, u32[]{:S(2)}) async-start(bf16[16,2,5120]{2,1,0:T(2,128)(2,1)} %reshape.302), calls=%async_computation.2 | async-start | bytes 655360 | tf_op jit(solution)/shard_map/all_to_all | solution.py:195
  239.1 1.3 dynamic-slice
  241.0 52.4 %all-reduce.5.cloned.1.call-done = bf16[5120,2,128]{2,1,0:T(2,128)(2,1)} async-done(((bf16[5120,2,128]{2,1,0:T(2,128)(2,1)}), bf16[5120,2,128]{2,1,0:T(2,128)(2,1)}) %all-reduce.5.cloned.1.call-update) | async-done | bytes 2621456
  293.4 2.2 constant_dynamic-slice_fusion.1
  295.6 1.3 dynamic-slice.2
  297.5 91.8 %all-reduce.7.cloned.1.call-done = bf16[1280,2,128]{2,1,0:T(2,128)(2,1)} async-done(((bf16[1280,2,128]{2,1,0:T(2,128)(2,1)}), bf16[1280,2,128]{2,1,0:T(2,128)(2,1)}) %all-reduce.7.cloned.1.call-update) | async-done | bytes 655376
  389.3 1.0 constant_dynamic-slice_fusion
  390.4 1.2 broadcast_in_dim.31
  391.6 5.3 %all-to-all-start.1 = ((f32[4,320,2,128]{3,1,2,0:T(8,128)}), f32[4,320,2,128]{3,1,2,0:T(8,128)S(1)}, u32[]{:S(2)}, u32[]{:S(2)}) async-start(f32[4,320,2,128]{3,1,2,0:T(8,128)} %broadcast_in_dim.31), calls=%async_computation.1 | async-start | bytes 2621440 | tf_op jit(solution)/shard_map/all_to_all | solution.py:27
  396.9 7.2 %reshape.303 = bf16[5120,4,8]{2,1,0:T(4,128)(2,1)} reshape(bf16[16,2,5120]{2,1,0:T(2,128)(2,1)S(1)} %all-to-all-done.2) | data formatting | bytes 655360
  404.1 7.0 %copy.171 = bf16[8,4,16,320]{3,1,0,2:T(4,128)(2,1)S(1)} copy(bf16[8,4,16,320]{0,1,3,2:T(4,128)(2,1)} %bitcast.236) | data formatting | bytes 655360 | tf_op jit(solution)/shard_map/all_to_all | solution.py:195
  411.1 0.2 reshape.279
  411.4 2.6 all-to-all-done.1
  413.9 0.1 reduce_sum.106
  414.0 0.3 convert_bitcast_fusion
  414.3 0.3 convolution_bitcast_fusion
  414.7 0.2 copy.172
  414.9 0.9 reshape_reshape.3
  415.8 6.7 %all-to-all-start.3 = ((f32[16,8,4,256]{3,2,1,0:T(4,128)}), f32[16,8,4,256]{3,2,1,0:T(4,128)S(1)}, u32[]{:S(2)}, u32[]{:S(2)}) async-start(f32[16,8,4,256]{3,2,1,0:T(4,128)} %reshape_reshape.3), calls=%async_computation.3 | async-start | bytes 1048576 | tf_op jit(solution)/shard_map/all_to_all | solution.py:51
  422.6 1.4 copy.229
  424.1 0.4 fusion.74
  424.4 1.0 copy.178
  425.4 1.0 copy.179
  426.4 1.0 copy.180
  427.4 26.3 %all-to-all-done.3 = f32[16,8,4,256]{3,2,1,0:T(4,128)S(1)} async-done(((f32[16,8,4,256]{3,2,1,0:T(4,128)}), f32[16,8,4,256]{3,2,1,0:T(4,128)S(1)}, u32[]{:S(2)}, u32[]{:S(2)}) %all-to-all-start.3) | async-done | bytes 524320 | tf_op jit(solution)/shard_map/all_to_all | solution.py:51
  453.7 0.1 reduce_sum.107
  453.9 0.4 fusion.75
  454.3 0.2 fusion.53
  454.6 0.2 fusion.61
  454.8 0.3 fusion.46
  455.1 0.7 reshape.296
  (39 shorter events, 0.7 us)
Async XLA Ops:
  7.2 114.8 %all-gather.5.cloned.1.call-start = ((), (), s32[]{:S(2)}) async-start(), calls=%async_computation.5 | async-start | bytes 2785280 | tf_op jit(solution)/shard_map/all_gather | solution.py:146
  9.0 179.0 %all-gather.3.cloned.1.call-start = ((), (), s32[]{:S(2)}) async-start(), calls=%async_computation.4 | async-start | bytes 5898240 | tf_op jit(solution)/shard_map/all_gather | solution.py:147
  12.6 37.3 %all-to-all-start = ((f32[64,1,128]{2,1,0:T(1,128)}), f32[64,1,128]{2,1,0:T(1,128)S(1)}, u32[]{:S(2)}, u32[]{:S(2)}) async-start(f32[64,1,128]{2,1,0:T(1,128)} %reshape.300), calls=%async_computation | async-start | bytes 65536 | tf_op jit(solution)/shard_map/all_to_all | solution.py:27
  34.4 259.0 %all-reduce.5.cloned.1.call-start = ((), (), s32[]{:S(2)}) async-start(), calls=%async_computation.6 | async-start | bytes 5242880
  196.7 4.4 slice-start
  198.6 2.5 slice-start.1
  202.8 4.8 %copy-start.3 = (bf16[8,4,5120]{2,1,0:T(4,128)(2,1)S(1)}, bf16[8,4,5120]{2,1,0:T(4,128)(2,1)}, u32[]{:S(2)}) copy-start(bf16[8,4,5120]{2,1,0:T(4,128)(2,1)} %param.24) | copy-start | bytes 983044
  224.8 165.6 %all-to-all-start.2 = ((bf16[16,2,5120]{2,1,0:T(2,128)(2,1)}), bf16[16,2,5120]{2,1,0:T(2,128)(2,1)S(1)}, u32[]{:S(2)}, u32[]{:S(2)}) async-start(bf16[16,2,5120]{2,1,0:T(2,128)(2,1)} %reshape.302), calls=%async_computation.2 | async-start | bytes 655360 | tf_op jit(solution)/shard_map/all_to_all | solution.py:195
  239.0 150.3 %all-reduce.7.cloned.1.call-start = ((), (), s32[]{:S(2)}) async-start(), calls=%async_computation.7 | async-start | bytes 1310720
  391.6 22.3 %all-to-all-start.1 = ((f32[4,320,2,128]{3,1,2,0:T(8,128)}), f32[4,320,2,128]{3,1,2,0:T(8,128)S(1)}, u32[]{:S(2)}, u32[]{:S(2)}) async-start(f32[4,320,2,128]{3,1,2,0:T(8,128)} %broadcast_in_dim.31), calls=%async_computation.1 | async-start | bytes 2621440 | tf_op jit(solution)/shard_map/all_to_all | solution.py:27
  404.1 9.9 %copy-start = (f32[320,2,128]{2,1,0:T(2,128)S(1)}, f32[320,2,128]{2,1,0:T(2,128)}, u32[]{:S(2)}) copy-start(f32[320,2,128]{2,1,0:T(2,128)} %param.21) | copy-start | bytes 983044
  404.1 9.9 %copy-start.1 = (f32[320,2,128]{2,1,0:T(2,128)S(1)}, f32[320,2,128]{2,1,0:T(2,128)}, u32[]{:S(2)}) copy-start(f32[320,2,128]{2,1,0:T(2,128)} %param.22) | copy-start | bytes 983044
  404.1 9.9 %copy-start.2 = (f32[320,2,128]{2,1,0:T(2,128)S(1)}, f32[320,2,128]{2,1,0:T(2,128)}, u32[]{:S(2)}) copy-start(f32[320,2,128]{2,1,0:T(2,128)} %param.23) | copy-start | bytes 983044
  411.1 11.4 %copy-start.4 = (bf16[8,4,640]{2,1,0:T(4,128)(2,1)S(1)}, bf16[8,4,640]{2,1,0:T(4,128)(2,1)}, u32[]{:S(2)}) copy-start(bf16[8,4,640]{2,1,0:T(4,128)(2,1)} %param.25) | copy-start | bytes 122884
  411.3 12.7 %copy-start.5 = (s32[8]{0:T(128)S(1)}, s32[8]{0:T(128)}, u32[]{:S(2)}) copy-start(s32[8]{0:T(128)} %param.27) | copy-start | bytes 100
  415.8 37.9 %all-to-all-start.3 = ((f32[16,8,4,256]{3,2,1,0:T(4,128)}), f32[16,8,4,256]{3,2,1,0:T(4,128)S(1)}, u32[]{:S(2)}, u32[]{:S(2)}) async-start(f32[16,8,4,256]{3,2,1,0:T(4,128)} %reshape_reshape.3), calls=%async_computation.3 | async-start | bytes 1048576 | tf_op jit(solution)/shard_map/all_to_all | solution.py:51
Sparse Core Ops, SparseCore 0:
  11.6 110.3 all-gather.4
  124.1 63.8 all-gather.2
  207.6 85.7 all-reduce.4
  296.2 93.0 all-reduce.6
where the time goes:
time: 463 us; the launch traced here: 462 us
  waiting for transfers between devices  320 us (69%)
  local copies, waits for them, and re-layouts  53.6 us (12%)
  starting transfers between devices  48.1 us (10%)
  between operations  15.4 us (3%)
  matrix products  15.2 us (3%)
  other arithmetic  10.1 us (2%)
    unnamed x6, waiting for transfers between devices  145 us
    all_gather x1, waiting for transfers between devices, body(): weight_full = lax.all_gather(weight_low, FSDP, axis=0, tiled=True)  68.1 us
    all_gather x1, waiting for transfers between devices, body(): tokens_full = lax.all_gather(hidden, 'tensor', axis=1, tiled=True)  66 us
    unnamed x32, local copies, waits for them, and re-layouts  38.2 us
    all_to_all x2, starting transfers between devices, from_everyone(): lax.all_to_all(jnp.broadcast_to(shard[None], (count, *shard.shape)), axis...  27 us
    all_to_all x1, waiting for transfers between devices, summed_on_arrival(): lax.all_to_all(pieces, axis, split_axis=0, concat_axis=0, tiled=True)  26.3 us
    all_to_all x2, waiting for transfers between devices, from_everyone(): lax.all_to_all(jnp.broadcast_to(shard[None], (count, *shard.shape)), axis...  14.4 us
    all_to_all x1, starting transfers between devices, body(): lax.all_to_all(dec_hidden, FSDP, split_axis=2, concat_axis=0, tiled=True)  14.2 us
  transfers between devices with their start and end apart: 8, of which 7 were waited for; matrix products, arithmetic and copies ran while one was open for 11% of the time, Pallas kernels for 0%

commit v1 on v0

--- a/solution.py
+++ b/solution.py
@@ -143,7 +143,10 @@
     heads_here = kv_width // HD
     head_ratio = QH // KVH
     weight_low = kv_weight.astype(jnp.bfloat16)
-    weight_full = lax.all_gather(weight_low, FSDP, axis=0, tiled=True)
+    count_2 = lax.axis_size(FSDP)
+    tiles = jnp.stack([weight_low for _ in range(count_2)])
+    tiles = lax.all_to_all(tiles, FSDP, split_axis=0, concat_axis=0)
+    weight_full = jnp.concatenate(tiles, axis=0)
     tokens_full = lax.all_gather(hidden, "tensor", axis=1, tiled=True)
     projected = jnp.dot(
         tokens_full, weight_full.reshape(D, 2 * kv_width), preferred_element_type=jnp.float32

time: 463 us -> 492 us (1.063)
  waiting for transfers between devices: 320 us -> 338 us
  local copies, waits for them, and re-layouts: 53.6 us -> 59.4 us
    all_gather x1, waiting for transfers between devices: 66 us -> 151 us  [body(): tokens_full = lax.all_gather(hidden, 'tensor', axis=1, tiled=True)]
    all_gather x1 -> x0, waiting for transfers between devices: 68.1 us -> none  [body(): weight_full = lax.all_gather(weight_low, FSDP, axis=0, tiled=True)]
    unnamed x32 -> x44, local copies, waits for them, and re-layouts: 38.2 us -> 40.5 us
    unnamed x6 -> x5, waiting for transfers between devices: 145 us -> 143 us
  transfers between devices with their start and end apart: 8 -> 8, of which waited for: 7 -> 6; matrix products, arithmetic and copies ran while one was open for 11% -> 11% of each run, Pallas kernels for 0% -> 0%
where the time goes in v1:
time: 492 us; the launch traced here: 490 us
  waiting for transfers between devices  338 us (69%)
  local copies, waits for them, and re-layouts  59.4 us (12%)
  starting transfers between devices  52.4 us (11%)
  between operations  15.5 us (3%)
  matrix products  14.3 us (3%)
  other arithmetic  10.8 us (2%)
    all_gather x1, waiting for transfers between devices, body(): tokens_full = lax.all_gather(hidden, 'tensor', axis=1, tiled=True)  151 us
    unnamed x5, waiting for transfers between devices  143 us
    unnamed x44, local copies, waits for them, and re-layouts  40.5 us
    all_to_all x2, starting transfers between devices, from_everyone(): lax.all_to_all(jnp.broadcast_to(shard[None], (count, *shard.shape)), axis...  26.7 us
    all_to_all x1, waiting for transfers between devices, summed_on_arrival(): lax.all_to_all(pieces, axis, split_axis=0, concat_axis=0, tiled=True)  26.3 us
    all_to_all x2, waiting for transfers between devices, from_everyone(): lax.all_to_all(jnp.broadcast_to(shard[None], (count, *shard.shape)), axis...  16.7 us
    all_to_all x1, starting transfers between devices, body(): lax.all_to_all(dec_hidden, FSDP, split_axis=2, concat_axis=0, tiled=True)  14.3 us
  transfers between devices with their start and end apart: 8, of which 6 were waited for; matrix products, arithmetic and copies ran while one was open for 11% of the time, Pallas kernels for 0%

profile of v1, /device:TPU:1, one launch (start us, length us, event | category | flops | bytes accessed | tf_op | source)
XLA Modules:
  0.0 490.3 jit_solution(13916811741073370475)
XLA Ops:
  7.2 0.7 multiply_bitcast_fusion.1
  7.8 0.7 and_select_fusion
  8.6 0.7 pad_maximum_fusion.1
  9.2 0.1 multiply_reduce_fusion
  9.3 0.7 reshape.298
  10.1 21.7 %all-to-all-start.1 = ((f32[64,1,128]{2,1,0:T(1,128)}), f32[64,1,128]{2,1,0:T(1,128)S(1)}, u32[]{:S(2)}, u32[]{:S(2)}) async-start(f32[64,1,128]{2,1,0:T(1,128)} %reshape.298), calls=%async_computation.1 | async-start | bytes 65536 | tf_op jit(solution)/shard_map/all_to_all | solution.py:27
  31.8 1.1 convert_element_type.98
  32.9 14.4 %all-to-all-done.1 = f32[64,1,128]{2,1,0:T(1,128)S(1)} async-done(((f32[64,1,128]{2,1,0:T(1,128)}), f32[64,1,128]{2,1,0:T(1,128)S(1)}, u32[]{:S(2)}, u32[]{:S(2)}) %all-to-all-start.1) | async-done | bytes 32800 | tf_op jit(solution)/shard_map/all_to_all | solution.py:27
  47.4 3.5 stack.14
  50.9 3.7 all-to-all-start
  54.7 0.7 all-gather.2.cloned.1.call-update
  55.4 1.3 copy.154
  56.8 2.2 copy.157
  59.0 0.2 fusion.49
  59.2 0.5 broadcast.180
  59.7 2.1 reduce.7
  61.8 1.5 reshape.299
  63.3 0.9 bitcast_reduce_fusion
  64.2 0.2 select_reduce_fusion.2
  64.4 0.1 select_reduce_fusion
  64.5 2.1 multiply_convert_fusion.1
  66.6 151.3 %all-gather.2.cloned.1.call-done = bf16[512,5120]{1,0:T(8,128)(2,1)} async-done(((bf16[512,640]{1,0:T(8,128)(2,1)}), bf16[512,5120]{1,0:T(8,128)(2,1)}) %all-gather.2.cloned.1.call-update) | async-done | bytes 5242896 | tf_op jit(solution)/shard_map/all_gather | solution.py:150
  217.9 4.0 fusion.20
  222.0 1.1 fusion.6
  223.1 1.1 fusion.5
  224.2 1.7 fusion.39
  225.9 1.9 fusion
  227.8 2.4 fusion.42
  230.3 1.6 convolution_convert_fusion
  232.0 4.7 copy.161
  236.7 5.0 %copy.170 = bf16[8,4,5120]{0,1,2:T(4,128)(2,1)} copy(bf16[8,4,5120]{2,1,0:T(4,128)(2,1)S(1)} %copy-done.5) | data formatting | bytes 655360 | tf_op args[10]
  241.7 12.3 %reshape.300 = bf16[16,2,5120]{2,1,0:T(2,128)(2,1)} reshape(bf16[5120,4,8]{2,1,0:T(4,128)(2,1)} %bitcast.238) | data formatting | bytes 655360
  254.0 14.3 %all-to-all-start.3 = ((bf16[16,2,5120]{2,1,0:T(2,128)(2,1)}), bf16[16,2,5120]{2,1,0:T(2,128)(2,1)S(1)}, u32[]{:S(2)}, u32[]{:S(2)}) async-start(bf16[16,2,5120]{2,1,0:T(2,128)(2,1)} %reshape.300), calls=%async_computation.3 | async-start | bytes 655360 | tf_op jit(solution)/shard_map/all_to_all | solution.py:198
  268.3 1.3 dynamic-slice
  270.2 50.7 %all-reduce.5.cloned.1.call-done = bf16[5120,2,128]{2,1,0:T(2,128)(2,1)} async-done(((bf16[5120,2,128]{2,1,0:T(2,128)(2,1)}), bf16[5120,2,128]{2,1,0:T(2,128)(2,1)}) %all-reduce.5.cloned.1.call-update) | async-done | bytes 2621456
  321.0 2.2 constant_dynamic-slice_fusion.1
  323.2 1.3 dynamic-slice.2
  325.1 92.0 %all-reduce.7.cloned.1.call-done = bf16[1280,2,128]{2,1,0:T(2,128)(2,1)} async-done(((bf16[1280,2,128]{2,1,0:T(2,128)(2,1)}), bf16[1280,2,128]{2,1,0:T(2,128)(2,1)}) %all-reduce.7.cloned.1.call-update) | async-done | bytes 655376
  417.1 1.0 constant_dynamic-slice_fusion
  418.2 1.2 broadcast_in_dim.31
  419.4 4.9 %all-to-all-start.2 = ((f32[4,320,2,128]{3,1,2,0:T(8,128)}), f32[4,320,2,128]{3,1,2,0:T(8,128)S(1)}, u32[]{:S(2)}, u32[]{:S(2)}) async-start(f32[4,320,2,128]{3,1,2,0:T(8,128)} %broadcast_in_dim.31), calls=%async_computation.2 | async-start | bytes 2621440 | tf_op jit(solution)/shard_map/all_to_all | solution.py:27
  424.3 7.2 %reshape.301 = bf16[5120,4,8]{2,1,0:T(4,128)(2,1)} reshape(bf16[16,2,5120]{2,1,0:T(2,128)(2,1)S(1)} %all-to-all-done.3) | data formatting | bytes 655360
  431.5 7.0 %copy.171 = bf16[8,4,16,320]{3,1,0,2:T(4,128)(2,1)S(1)} copy(bf16[8,4,16,320]{0,1,3,2:T(4,128)(2,1)} %bitcast.237) | data formatting | bytes 655360 | tf_op jit(solution)/shard_map/all_to_all | solution.py:198
  438.5 0.2 reshape.277
  438.7 2.3 all-to-all-done.2
  441.0 0.1 reduce_sum.106
  441.1 0.3 convert_bitcast_fusion
  441.4 0.3 convolution_bitcast_fusion
  441.8 0.2 copy.172
  442.0 0.9 reshape_reshape.7
  442.9 7.6 %all-to-all-start.4 = ((f32[16,8,4,256]{3,2,1,0:T(4,128)}), f32[16,8,4,256]{3,2,1,0:T(4,128)S(1)}, u32[]{:S(2)}, u32[]{:S(2)}) async-start(f32[16,8,4,256]{3,2,1,0:T(4,128)} %reshape_reshape.7), calls=%async_computation.4 | async-start | bytes 1048576 | tf_op jit(solution)/shard_map/all_to_all | solution.py:51
  450.6 1.4 copy.229
  452.1 0.4 fusion.74
  452.5 1.0 copy.178
  453.5 1.0 copy.179
  454.4 1.0 copy.180
  455.4 26.3 %all-to-all-done.4 = f32[16,8,4,256]{3,2,1,0:T(4,128)S(1)} async-done(((f32[16,8,4,256]{3,2,1,0:T(4,128)}), f32[16,8,4,256]{3,2,1,0:T(4,128)S(1)}, u32[]{:S(2)}, u32[]{:S(2)}) %all-to-all-start.4) | async-done | bytes 524320 | tf_op jit(solution)/shard_map/all_to_all | solution.py:51
  481.7 0.1 reduce_sum.107
  481.9 0.4 fusion.75
  482.3 0.2 fusion.53
  482.5 0.1 fusion.60
  482.6 0.2 fusion.61
  482.9 0.3 fusion.46
  483.2 0.7 reshape.294
  (51 shorter events, 0.6 us)
Async XLA Ops:
  10.1 37.3 %all-to-all-start.1 = ((f32[64,1,128]{2,1,0:T(1,128)}), f32[64,1,128]{2,1,0:T(1,128)S(1)}, u32[]{:S(2)}, u32[]{:S(2)}) async-start(f32[64,1,128]{2,1,0:T(1,128)} %reshape.298), calls=%async_computation.1 | async-start | bytes 65536 | tf_op jit(solution)/shard_map/all_to_all | solution.py:27
  32.9 26.1 %copy-start.8 = (s32[1,512]{1,0:T(1,128)S(1)}, s32[1,512]{1,0:T(1,128)}, u32[]{:S(2)}) copy-start(s32[1,512]{1,0:T(1,128)} %param.17) | copy-start | bytes 6148
  32.9 31.5 %copy-start.10 = (f32[16]{0:T(128)S(1)}, f32[16]{0:T(128)}, u32[]{:S(2)}) copy-start(f32[16]{0:T(128)} %param.19) | copy-start | bytes 196
  32.9 31.6 %copy-start.9 = (s32[512]{0:T(512)S(1)}, s32[512]{0:T(512)}, u32[]{:S(2)}) copy-start(s32[512]{0:T(512)} %param.18) | copy-start | bytes 6148
  47.4 8.0 %copy-start.6 = (f32[64,1,128]{2,1,0:T(1,128)}, f32[64,1,128]{2,1,0:T(1,128)S(1)}, u32[]{:S(2)}) copy-start(f32[64,1,128]{2,1,0:T(1,128)S(1)} %all-to-all-done.1) | copy-start | bytes 98308
  50.9 167.0 %all-to-all-start = ((bf16[16,320,2,128]{3,2,1,0:T(2,128)(2,1)}), bf16[16,320,2,128]{3,2,1,0:T(2,128)(2,1)S(1)}, u32[]{:S(2)}, u32[]{:S(2)}) async-start(bf16[16,320,2,128]{3,2,1,0:T(2,128)(2,1)} %stack.14), calls=%async_computation | async-start | bytes 5242880 | tf_op jit(solution)/shard_map/all_to_all | solution.py:148
  54.6 163.3 %all-gather.2.cloned.1.call-start = ((), (), s32[]{:S(2)}) async-start(), calls=%async_computation.5 | async-start | bytes 5898240 | tf_op jit(solution)/shard_map/all_gather | solution.py:150
  55.4 265.6 %all-reduce.5.cloned.1.call-start = ((), (), s32[]{:S(2)}) async-start(), calls=%async_computation.6 | async-start | bytes 5242880
  222.0 2.2 copy-start
  224.2 1.7 copy-start.2
  225.9 4.4 slice-start
  227.8 2.5 slice-start.1
  231.9 4.8 copy-start.5
  254.0 164.2 %all-to-all-start.3 = ((bf16[16,2,5120]{2,1,0:T(2,128)(2,1)}), bf16[16,2,5120]{2,1,0:T(2,128)(2,1)S(1)}, u32[]{:S(2)}, u32[]{:S(2)}) async-start(bf16[16,2,5120]{2,1,0:T(2,128)(2,1)} %reshape.300), calls=%async_computation.3 | async-start | bytes 655360 | tf_op jit(solution)/shard_map/all_to_all | solution.py:198
  268.3 148.8 %all-reduce.7.cloned.1.call-start = ((), (), s32[]{:S(2)}) async-start(), calls=%async_computation.7 | async-start | bytes 1310720
  419.4 21.7 %all-to-all-start.2 = ((f32[4,320,2,128]{3,1,2,0:T(8,128)}), f32[4,320,2,128]{3,1,2,0:T(8,128)S(1)}, u32[]{:S(2)}, u32[]{:S(2)}) async-start(f32[4,320,2,128]{3,1,2,0:T(8,128)} %broadcast_in_dim.31), calls=%async_computation.2 | async-start | bytes 2621440 | tf_op jit(solution)/shard_map/all_to_all | solution.py:27
  431.5 9.6 %copy-start.1 = (f32[320,2,128]{2,1,0:T(2,128)S(1)}, f32[320,2,128]{2,1,0:T(2,128)}, u32[]{:S(2)}) copy-start(f32[320,2,128]{2,1,0:T(2,128)} %param.21) | copy-start | bytes 983044
  431.5 9.6 %copy-start.3 = (f32[320,2,128]{2,1,0:T(2,128)S(1)}, f32[320,2,128]{2,1,0:T(2,128)}, u32[]{:S(2)}) copy-start(f32[320,2,128]{2,1,0:T(2,128)} %param.22) | copy-start | bytes 983044
  431.5 9.6 %copy-start.4 = (f32[320,2,128]{2,1,0:T(2,128)S(1)}, f32[320,2,128]{2,1,0:T(2,128)}, u32[]{:S(2)}) copy-start(f32[320,2,128]{2,1,0:T(2,128)} %param.23) | copy-start | bytes 983044
  438.5 12.0 %copy-start.7 = (bf16[8,4,640]{2,1,0:T(4,128)(2,1)S(1)}, bf16[8,4,640]{2,1,0:T(4,128)(2,1)}, u32[]{:S(2)}) copy-start(bf16[8,4,640]{2,1,0:T(4,128)(2,1)} %param.25) | copy-start | bytes 122884
  438.7 13.3 %copy-start.11 = (s32[8]{0:T(128)S(1)}, s32[8]{0:T(128)}, u32[]{:S(2)}) copy-start(s32[8]{0:T(128)} %param.27) | copy-start | bytes 100
  442.9 38.8 %all-to-all-start.4 = ((f32[16,8,4,256]{3,2,1,0:T(4,128)}), f32[16,8,4,256]{3,2,1,0:T(4,128)S(1)}, u32[]{:S(2)}, u32[]{:S(2)}) async-start(f32[16,8,4,256]{3,2,1,0:T(4,128)} %reshape_reshape.7), calls=%async_computation.4 | async-start | bytes 1048576 | tf_op jit(solution)/shard_map/all_to_all | solution.py:51
Sparse Core Ops, SparseCore 0:
  57.5 160.3 all-gather.1
  236.8 84.1 all-reduce.4
  323.9 93.1 all-reduce.6
